TPU v7x, 32 devices: a whole 2x2x4 slice. The times are simulated.
32 devices in a mesh: row: 4 (over y, core), phi: 8 (over z, x).
Axes of the slice: x: 2, y: 2, z: 4, core: 2. Of those that a mesh axis runs over, the one named last changes fastest.
Arguments:
- hydro_vars: float32 [5, 128, 128, 256], P(None, 'row', 'phi'), may hold values from -6 to 6
- face_b: float32 [3, 128, 128, 256], P(None, 'row', 'phi'), may hold values from -6 to 6
- widths: int32 [16], replicated, may hold values from 2 to 128, as said below
- diffusion: float32 [5, 256], replicated, may hold values from 0.01 to 0.06
Outputs:
- conserved: float32 [8, 128, 128, 256], P(None, 'row', 'phi')
- faces_out: float32 [3, 128, 128, 256], P(None, 'row', 'phi')
Inputs may be any that keep to these rules, and one draw needn't show every extreme that they name: `widths`: every width is a power of two that divides 128; the two cycles next to the poles (entries 0 and 15) use 128.
All inputs are finite; a program needn't handle non-finite values.
Results may differ from a plain program's by a relative error of at most 0.0001.
Values sent between devices are 32-bit elements; how exact they have to be, the bound alone decides.
A program may use at most 64 MiB of HBM per device.

v0:
```python
import jax
import jax.numpy as jnp
from jax import lax
from jax.sharding import PartitionSpec as P

CYCLES = 8


def extended(cells, sides, width, closed):
    for axis, dim in sides:
        count = lax.axis_size(axis)
        ends = count if closed else count - 1
        head = lax.slice_in_dim(cells, 0, width, axis=dim)
        tail = lax.slice_in_dim(cells, cells.shape[dim] - width, cells.shape[dim], axis=dim)
        cells = jnp.concatenate(
            [
                lax.ppermute(tail, axis, [(i, (i + 1) % count) for i in range(ends)]),
                cells,
                lax.ppermute(head, axis, [((i + 1) % count, i) for i in range(ends)]),
            ],
            axis=dim,
        )
    return cells


def passed_along(value, axis, steps):
    count = lax.axis_size(axis)
    initial, last = (max(0, -steps), min(count, count - steps))
    return lax.ppermute(value, axis, [(source, source + steps) for source in range(initial, last)])


def passed_along_2(block, axis, distance):
    devices = range(lax.axis_size(axis))
    route = [((i - distance) % len(devices), i) for i in devices]
    return lax.ppermute(block, axis, route)


def stencil(padded, axis, count):
    parts = [lax.slice_in_dim(padded, offset, offset + count, axis=axis) for offset in range(5)]
    return (16.0 * (parts[1] + parts[3]) - (parts[0] + parts[4]) - 30.0 * parts[2]) / 12.0


def block_means(cycles, axis, width, limit):
    cells = cycles.shape[axis]
    result = cycles
    for power in range(1, limit.bit_length()):
        size = 2**power
        shape = cycles.shape[:axis] + (cells // size, size) + cycles.shape[axis + 1 :]
        means = jnp.mean(cycles.reshape(shape), axis=axis + 1, keepdims=True)
        means = jnp.broadcast_to(means, shape).reshape(cycles.shape)
        result = jnp.where(width == size, means, result)
    return result


def body(hydro_vars, face_b, widths, diffusion):
    fields = jnp.concatenate([hydro_vars, face_b], 0)
    nfield, rows, cells, theta_cells = fields.shape
    cycle_count = 2 * CYCLES
    polar_cycles = jnp.concatenate([fields[..., :CYCLES], fields[..., theta_cells - CYCLES :]], 3)
    slab = polar_cycles.transpose(2, 0, 1, 3).reshape(cells, nfield * rows * cycle_count)
    whole = lax.all_to_all(slab, "phi", split_axis=1, concat_axis=0, tiled=True)
    columns = whole.shape[1]
    first = lax.axis_index("phi") * columns
    cycle_of = (first + jnp.arange(columns, dtype=jnp.int32)) % cycle_count
    match = cycle_of[:, None] == jnp.arange(cycle_count, dtype=jnp.int32)[None, :]
    column_width = jnp.sum(jnp.where(match, widths[None, :], 0), axis=1)
    means = block_means(whole, 0, column_width[None, :], whole.shape[0])
    back = lax.all_to_all(means, "phi", split_axis=0, concat_axis=1, tiled=True)
    averaged = back.reshape(cells, nfield, rows, cycle_count).transpose(1, 2, 0, 3)
    fields = jnp.concatenate(
        [
            averaged[..., :CYCLES],
            fields[..., CYCLES : theta_cells - CYCLES],
            averaged[..., CYCLES:],
        ],
        3,
    )
    hydro = fields[:5]
    radial_pad = extended(hydro, (("row", 1),), 2, False)
    azimuth_pad = extended(hydro, (("phi", 2),), 2, True)
    change_radial = stencil(radial_pad, 1, rows)
    change_azimuth = stencil(azimuth_pad, 2, cells)
    outer_layer = passed_along(fields[5, :1], "row", -1)
    radial_next = jnp.concatenate([fields[5, 1:], outer_layer], 0)
    after_layer = passed_along_2(fields[7, :, :1], "phi", -1)
    azimuth_next = jnp.concatenate([fields[7, :, 1:], after_layer], 1)
    theta_pad = jnp.pad(hydro, ((0, 0), (0, 0), (0, 0), (2, 2)))
    change = change_radial + change_azimuth + stencil(theta_pad, 3, theta_cells)
    smoothed = hydro + diffusion[:, None, None, :] * change
    polar_face = fields[6]
    polar_next = jnp.concatenate([polar_face[..., 1:], jnp.zeros_like(polar_face[..., :1])], 2)
    cell_field = 0.5 * jnp.stack(
        [fields[5] + radial_next, polar_face + polar_next, fields[7] + azimuth_next]
    )
    return (jnp.concatenate([smoothed, cell_field], 0), fields[5:])


def solution(mesh):
    in_specs = (P(None, "row", "phi", None), P(None, "row", "phi", None), P(), P())
    out_specs = (P(None, "row", "phi", None), P(None, "row", "phi", None))
    return jax.shard_map(body, mesh=mesh, in_specs=in_specs, out_specs=out_specs, check_vma=False)
```

profile of v0, /device:TPU:0, one launch (start us, length us, event | category | flops | bytes accessed | tf_op | source)
XLA Modules:
  0.0 84.1 jit_solution(16778632475743452020)
XLA Ops:
  0.6 2.1 %constant_dynamic-update-slice_fusion.1 = f32[8,32,16,256]{3,2,1,0:T(8,128)S(1)} fusion(f32[5,32,16,256]{3,2,1,0:T(8,128)} %param.4), kind=kLoop, calls=%fused_computation.65 | loop fusion | bytes 5242880
  3.0 0.7 fusion.27
  3.7 1.3 %copy-done.2 = f32[8,32,16,256]{3,2,1,0:T(8,128)} copy-done((f32[8,32,16,256]{3,2,1,0:T(8,128)}, f32[8,32,16,256]{3,2,1,0:T(8,128)S(1)}, u32[]{:S(2)}) %copy-start.2) | copy-done | bytes 4194328
  5.0 0.6 maximum_bitcast_fusion
  5.6 0.6 copy.46
  6.2 2.3 %reshape.192 = f32[16,8,512]{2,0,1:T(8,128)} reshape(f32[16,8,32,16]{3,2,0,1:T(8,128)S(1)} %copy.46) | data formatting | bytes 524288 | tf_op jit(solution)/shard_map/all_to_all | solution.py:61
  8.5 7.3 %all-to-all-start = ((f32[16,8,512]{2,0,1:T(8,128)}), f32[16,8,512]{2,0,1:T(8,128)S(1)}, u32[]{:S(2)}, u32[]{:S(2)}) async-start(f32[16,8,512]{2,0,1:T(8,128)} %reshape.192), calls=%async_computation | async-start | bytes 524288 | tf_op jit(solution)/shard_map/all_to_all | solution.py:61
  15.9 8.8 %all-to-all-done = f32[16,8,512]{2,0,1:T(8,128)S(1)} async-done(((f32[16,8,512]{2,0,1:T(8,128)}), f32[16,8,512]{2,0,1:T(8,128)S(1)}, u32[]{:S(2)}, u32[]{:S(2)}) %all-to-all-start) | async-done | bytes 262176 | tf_op jit(solution)/shard_map/all_to_all | solution.py:61
  25.3 0.3 reduce_sum.85
  26.3 0.8 %fusion.25 = f32[8,16,512]{2,1,0:T(8,128)} fusion(f32[8,16,512]{2,1,0:T(8,128)S(1)} %reshape.188, f32[8,16,512]{2,1,0:T(8,128)S(1)} %reshape.190, f32[8,512]{1,0:T(8,128)S(1)} %broadcast_multiply_fusion.3, f32[8,512]{1,0:T(8,128)S(1)} %broadcast_in_dim.113, f32[8,512]{1,0:T(8,128)S(1)} %broadcast_in_dim.109, f32[512]{0:T(512)S(1)} %broadcast_multiply_fusion.7, ...), kind=kLoop, calls=%fused_computation.53 | loop fusion | flops 458752 | bytes 1365504 | tf_op jit(solution)/shard_map/jit(_where)/select_n | solution.py:51
  27.1 3.6 %all-to-all-start.1 = ((f32[8,16,512]{2,1,0:T(8,128)}), f32[8,16,512]{2,1,0:T(8,128)S(1)}, u32[]{:S(2)}, u32[]{:S(2)}) async-start(f32[8,16,512]{2,1,0:T(8,128)} %fusion.25), calls=%async_computation.1 | async-start | bytes 524288 | tf_op jit(solution)/shard_map/all_to_all | solution.py:68
  30.7 5.3 %slice.140 = f32[8,32,16,240]{3,2,1,0:T(8,128)} slice(f32[8,32,16,256]{3,2,1,0:T(8,128)} %copy-done.2), slice={[0:8], [0:32], [0:16], [8:248]} | slice | bytes 7864320 | tf_op jit(solution)/shard_map/slice | solution.py:73
  36.0 3.3 %all-to-all-done.1 = f32[8,16,512]{2,1,0:T(8,128)S(1)} async-done(((f32[8,16,512]{2,1,0:T(8,128)}), f32[8,16,512]{2,1,0:T(8,128)S(1)}, u32[]{:S(2)}, u32[]{:S(2)}) %all-to-all-start.1) | async-done | bytes 262176 | tf_op jit(solution)/shard_map/all_to_all | solution.py:68
  39.4 0.7 reshape.191
  40.2 0.8 fusion.28
  40.9 1.2 %copy.40 = f32[8,32,16,8]{3,2,1,0:T(8,128)S(1)} copy(f32[8,32,16,8]{3,1,0,2:T(8,128)S(1)} %get-tuple-element.13) | data formatting | bytes 262144 | tf_op jit(solution)/shard_map/slice | solution.py:72
  42.1 1.2 %copy.41 = f32[8,32,16,8]{3,2,1,0:T(8,128)S(1)} copy(f32[8,32,16,8]{3,1,0,2:T(8,128)S(1)} %get-tuple-element.14) | data formatting | bytes 262144 | tf_op jit(solution)/shard_map/slice | solution.py:74
  43.3 1.0 %copy-done = f32[8,32,16,240]{3,2,1,0:T(8,128)S(1)} copy-done((f32[8,32,16,240]{3,2,1,0:T(8,128)S(1)}, f32[8,32,16,240]{3,2,1,0:T(8,128)}, u32[]{:S(2)}) %copy-start) | copy-done | bytes 3932184
  44.6 1.1 %pad_maximum_fusion.7 = (f32[5,32,2,256]{3,2,1,0:T(2,128)S(1)}, f32[5,32,2,256]{3,2,1,0:T(2,128)S(1)}) fusion(f32[8,32,16,8]{3,2,1,0:T(8,128)S(1)} %copy.41, f32[8,32,16,240]{3,2,1,0:T(8,128)S(1)} %copy-done, f32[8,32,16,8]{3,2,1,0:T(8,128)S(1)} %copy.40), kind=kLoop, calls=%fused_computation.48 | loop fusion | flops 327680 | bytes 4849664 | tf_op jit(solution)/shard_map/slice | solution.py:14
  45.7 1.7 %pad_maximum_fusion = f32[8,32,16,256]{3,2,1,0:T(8,128)S(1)} fusion(f32[8,32,16,8]{3,2,1,0:T(8,128)S(1)} %copy.41, f32[8,32,16,240]{3,2,1,0:T(8,128)S(1)} %copy-done, f32[8,32,16,8]{3,2,1,0:T(8,128)S(1)} %copy.40), kind=kLoop, calls=%fused_computation.4 | loop fusion | flops 2097152 | bytes 8388608 | tf_op jit(solution)/shard_map/concatenate | solution.py:70
  47.4 1.3 %collective-permute-start.4 = (f32[1,16,256]{2,1,0:T(8,128)S(1)}, f32[1,16,256]{2,1,0:T(8,128)S(1)}, u32[]{:S(2)}, u32[]{:S(2)}) collective-permute-start(f32[1,16,256]{2,1,0:T(8,128)S(1)} %maximum_bitcast_fusion.2), channel_id=1, source_target_pairs={{8,0},{16,8},{24,16},{9,1},{17,9},{25,17},{10,2},{18,10},{26,18},{... | collective-permute-start | bytes 49160 | tf_op jit(solution)/shard_map/ppermute | solution.py:29
  48.7 2.4 %collective-permute-start.5 = (f32[32,1,256]{2,1,0:T(1,128)S(1)}, f32[32,1,256]{2,1,0:T(1,128)S(1)}, u32[]{:S(2)}, u32[]{:S(2)}) collective-permute-start(f32[32,1,256]{2,1,0:T(1,128)S(1)} %maximum_bitcast_fusion.1), channel_id=1, source_target_pairs={{1,0},{2,1},{3,2},{4,3},{5,4},{6,5},{7,6},{0,7},{9,8},{10,9},{11,1... | collective-permute-start | bytes 98312 | tf_op jit(solution)/shard_map/ppermute | solution.py:35
  51.3 1.3 %slice.157 = f32[3,32,16,256]{3,2,1,0:T(8,128)} slice(f32[8,32,16,256]{3,2,1,0:T(8,128)S(1)} %pad_maximum_fusion), slice={[5:8], [0:32], [0:16], [0:256]} | slice | bytes 3145728 | tf_op jit(solution)/shard_map/slice | solution.py:95
  52.6 2.8 %collective-permute-start = (f32[5,2,16,256]{3,2,1,0:T(8,128)S(1)}, f32[5,2,16,256]{3,2,1,0:T(8,128)S(1)}, u32[]{:S(2)}, u32[]{:S(2)}) collective-permute-start(f32[5,2,16,256]{3,2,1,0:T(8,128)S(1)} %get-tuple-element.6), channel_id=1, source_target_pairs={{0,8},{8,16},{16,24},{1,9},{9,17},{17,25},{2,10},{10,18},{18,26},{... | collective-permute-start | bytes 491528 | tf_op jit(solution)/shard_map/ppermute | solution.py:17
  55.3 1.3 %collective-permute-start.1 = (f32[5,2,16,256]{3,2,1,0:T(8,128)S(1)}, f32[5,2,16,256]{3,2,1,0:T(8,128)}, u32[]{:S(2)}, u32[]{:S(2)}) collective-permute-start(f32[5,2,16,256]{3,2,1,0:T(8,128)S(1)} %get-tuple-element.7), channel_id=1, source_target_pairs={{8,0},{16,8},{24,16},{9,1},{17,9},{25,17},{10,2},{18,10},{26,18},{... | collective-permute-start | bytes 491528 | tf_op jit(solution)/shard_map/ppermute | solution.py:19
  56.7 0.3 collective-permute-start.3
  57.1 1.7 %collective-permute-start.2 = (f32[5,32,2,256]{3,1,2,0:T(8,128)S(1)}, f32[5,32,2,256]{3,1,2,0:T(8,128)S(1)}, u32[]{:S(2)}, u32[]{:S(2)}) collective-permute-start(f32[5,32,2,256]{3,1,2,0:T(8,128)S(1)} %copy.42), channel_id=1, source_target_pairs={{0,1},{1,2},{2,3},{3,4},{4,5},{5,6},{6,7},{7,0},{8,9},{9,10},{10,1... | collective-permute-start | bytes 983048 | tf_op jit(solution)/shard_map/ppermute | solution.py:17
  58.8 0.3 slice_add_fusion.1
  59.6 13.7 %collective-permute-done.3 = f32[5,32,2,256]{3,1,2,0:T(8,128)S(1)} collective-permute-done((f32[5,32,2,256]{3,1,2,0:T(8,128)S(1)}, f32[5,32,2,256]{3,1,2,0:T(8,128)S(1)}, u32[]{:S(2)}, u32[]{:S(2)}) %collective-permute-start.3) | collective-permute-done | bytes 327712 | tf_op jit(solution)/shard_map/ppermute | solution.py:19
  73.6 0.3 copy.43
  73.9 6.1 %fusion.8 = f32[5,32,16,256]{3,2,1,0:T(8,128)} fusion(f32[5,32,16,256]{3,2,1,0:T(8,128)S(1)} %slice-done, f32[5,2,16,256]{3,2,1,0:T(8,128)} %collective-permute-done.1, f32[5,2,16,256]{3,2,1,0:T(8,128)S(1)} %collective-permute-done, f32[5,32,2,256]{3,2,1,0:T(2,128)S(1)} %copy.45, f32[5,32,2,256]{3,2,1,0:T(2,128)S(1)} %copy.43, ...), kind=kLoop, calls=%fused_computation.22 | loop fusion | flops 18350080 | bytes 6231040 | tf_op jit(solution)/shard_map/add | solution.py:89
  79.9 4.2 %pad_maximum_fusion.1 = f32[8,32,16,256]{3,2,1,0:T(8,128)} fusion(f32[3,32,16,256]{3,2,1,0:T(8,128)S(1)} %maximum_multiply_fusion, f32[5,32,16,256]{3,2,1,0:T(8,128)} %fusion.8), kind=kLoop, calls=%fused_computation.5 | loop fusion | flops 1048576 | bytes 8388608 | tf_op jit(solution)/shard_map/concatenate | solution.py:95
  (60 shorter events, 2.9 us)
Async XLA Ops:
  0.6 2.2 %copy-start.3 = (f32[3,32,16,256]{3,2,1,0:T(8,128)S(1)}, f32[3,32,16,256]{3,2,1,0:T(8,128)}, u32[]{:S(2)}) copy-start(f32[3,32,16,256]{3,2,1,0:T(8,128)} %param.5) | copy-start | bytes 4718596
  2.9 2.0 %copy-start.2 = (f32[8,32,16,256]{3,2,1,0:T(8,128)}, f32[8,32,16,256]{3,2,1,0:T(8,128)S(1)}, u32[]{:S(2)}) copy-start(f32[8,32,16,256]{3,2,1,0:T(8,128)S(1)} %constant_dynamic-update-slice_fusion) | copy-start | bytes 12582916
  5.6 10.2 %copy-start.5 = (s32[16]{0:T(128)S(1)}, s32[16]{0:T(128)}, u32[]{:S(2)}) copy-start(s32[16]{0:T(128)} %param.6) | copy-start | bytes 196
  8.5 16.2 %all-to-all-start = ((f32[16,8,512]{2,0,1:T(8,128)}), f32[16,8,512]{2,0,1:T(8,128)S(1)}, u32[]{:S(2)}, u32[]{:S(2)}) async-start(f32[16,8,512]{2,0,1:T(8,128)} %reshape.192), calls=%async_computation | async-start | bytes 524288 | tf_op jit(solution)/shard_map/all_to_all | solution.py:61
  27.1 12.2 %all-to-all-start.1 = ((f32[8,16,512]{2,1,0:T(8,128)}), f32[8,16,512]{2,1,0:T(8,128)S(1)}, u32[]{:S(2)}, u32[]{:S(2)}) async-start(f32[8,16,512]{2,1,0:T(8,128)} %fusion.25), calls=%async_computation.1 | async-start | bytes 524288 | tf_op jit(solution)/shard_map/all_to_all | solution.py:68
  30.7 5.3 %copy-start.4 = (f32[5,256]{1,0:T(8,128)S(1)}, f32[5,256]{1,0:T(8,128)}, u32[]{:S(2)}) copy-start(f32[5,256]{1,0:T(8,128)} %param.7) | copy-start | bytes 15364
  42.1 2.2 %copy-start = (f32[8,32,16,240]{3,2,1,0:T(8,128)S(1)}, f32[8,32,16,240]{3,2,1,0:T(8,128)}, u32[]{:S(2)}) copy-start(f32[8,32,16,240]{3,2,1,0:T(8,128)} %slice.140) | copy-start | bytes 11796484
  47.3 12.0 %copy-start.1 = (f32[8,32,16,256]{3,2,1,0:T(8,128)}, f32[8,32,16,256]{3,2,1,0:T(8,128)S(1)}, u32[]{:S(2)}) copy-start(f32[8,32,16,256]{3,2,1,0:T(8,128)S(1)} %pad_maximum_fusion) | copy-start | bytes 12582916
  47.4 9.7 %collective-permute-start.4 = (f32[1,16,256]{2,1,0:T(8,128)S(1)}, f32[1,16,256]{2,1,0:T(8,128)S(1)}, u32[]{:S(2)}, u32[]{:S(2)}) collective-permute-start(f32[1,16,256]{2,1,0:T(8,128)S(1)} %maximum_bitcast_fusion.2), channel_id=1, source_target_pairs={{8,0},{16,8},{24,16},{9,1},{17,9},{25,17},{10,2},{18,10},{26,18},{... | collective-permute-start | bytes 49160 | tf_op jit(solution)/shard_map/ppermute | solution.py:29
  48.7 10.1 %collective-permute-start.5 = (f32[32,1,256]{2,1,0:T(1,128)S(1)}, f32[32,1,256]{2,1,0:T(1,128)S(1)}, u32[]{:S(2)}, u32[]{:S(2)}) collective-permute-start(f32[32,1,256]{2,1,0:T(1,128)S(1)} %maximum_bitcast_fusion.1), channel_id=1, source_target_pairs={{1,0},{2,1},{3,2},{4,3},{5,4},{6,5},{7,6},{0,7},{9,8},{10,9},{11,1... | collective-permute-start | bytes 98312 | tf_op jit(solution)/shard_map/ppermute | solution.py:35
  52.6 21.2 %collective-permute-start = (f32[5,2,16,256]{3,2,1,0:T(8,128)S(1)}, f32[5,2,16,256]{3,2,1,0:T(8,128)S(1)}, u32[]{:S(2)}, u32[]{:S(2)}) collective-permute-start(f32[5,2,16,256]{3,2,1,0:T(8,128)S(1)} %get-tuple-element.6), channel_id=1, source_target_pairs={{0,8},{8,16},{16,24},{1,9},{9,17},{17,25},{2,10},{10,18},{18,26},{... | collective-permute-start | bytes 491528 | tf_op jit(solution)/shard_map/ppermute | solution.py:17
  55.3 18.5 %collective-permute-start.1 = (f32[5,2,16,256]{3,2,1,0:T(8,128)S(1)}, f32[5,2,16,256]{3,2,1,0:T(8,128)}, u32[]{:S(2)}, u32[]{:S(2)}) collective-permute-start(f32[5,2,16,256]{3,2,1,0:T(8,128)S(1)} %get-tuple-element.7), channel_id=1, source_target_pairs={{8,0},{16,8},{24,16},{9,1},{17,9},{25,17},{10,2},{18,10},{26,18},{... | collective-permute-start | bytes 491528 | tf_op jit(solution)/shard_map/ppermute | solution.py:19
  56.7 16.6 %collective-permute-start.3 = (f32[5,32,2,256]{3,1,2,0:T(8,128)S(1)}, f32[5,32,2,256]{3,1,2,0:T(8,128)S(1)}, u32[]{:S(2)}, u32[]{:S(2)}) collective-permute-start(f32[5,32,2,256]{3,1,2,0:T(8,128)S(1)} %copy.44), channel_id=1, source_target_pairs={{1,0},{2,1},{3,2},{4,3},{5,4},{6,5},{7,6},{0,7},{9,8},{10,9},{11,1... | collective-permute-start | bytes 983048 | tf_op jit(solution)/shard_map/ppermute | solution.py:19
  57.1 16.5 %collective-permute-start.2 = (f32[5,32,2,256]{3,1,2,0:T(8,128)S(1)}, f32[5,32,2,256]{3,1,2,0:T(8,128)S(1)}, u32[]{:S(2)}, u32[]{:S(2)}) collective-permute-start(f32[5,32,2,256]{3,1,2,0:T(8,128)S(1)} %copy.42), channel_id=1, source_target_pairs={{0,1},{1,2},{2,3},{3,4},{4,5},{5,6},{6,7},{7,0},{8,9},{9,10},{10,1... | collective-permute-start | bytes 983048 | tf_op jit(solution)/shard_map/ppermute | solution.py:17
  59.4 14.4 %slice-start = ((f32[8,32,16,256]{3,2,1,0:T(8,128)}), f32[5,32,16,256]{3,2,1,0:T(8,128)S(1)}, s32[]{:S(2)}) async-start(f32[8,32,16,256]{3,2,1,0:T(8,128)} %copy-done.1), calls=%async_computation.2 | async-start | bytes 5242880 | tf_op jit(solution)/shard_map/slice | solution.py:78
where the time goes:
time: 85 us; the launch traced here: 84.1 us
  waiting for transfers between devices  25.8 us (30%)
  starting transfers between devices  20.7 us (24%)
  local copies, waits for them, and re-layouts  20.3 us (24%)
  other arithmetic  16.3 us (19%)
  between operations  1.09 us (1%)
    ppermute x2, waiting for transfers between devices, extended(): lax.ppermute(head, axis, [((i + 1) % count, i) for i in range(ends)])  13.7 us
    all_to_all x1, waiting for transfers between devices, body(): whole = lax.all_to_all(slab, 'phi', split_axis=1, concat_axis=0, tiled=True)  8.8 us
    all_to_all x1, starting transfers between devices, body(): whole = lax.all_to_all(slab, 'phi', split_axis=1, concat_axis=0, tiled=True)  7.28 us
    add x1, other arithmetic, body(): smoothed = hydro + diffusion[:, None, None, :] * change  6.07 us
    slice x1, local copies, waits for them, and re-layouts, body(): fields[..., CYCLES:theta_cells - CYCLES]  5.28 us
    ppermute x2, starting transfers between devices, extended(): lax.ppermute(tail, axis, [(i, (i + 1) % count) for i in range(ends)])  4.48 us
    unnamed x13, local copies, waits for them, and re-layouts  4.44 us
    concatenate x1, other arithmetic, body(): return (jnp.concatenate([smoothed, cell_field], 0), fields[5:])  4.2 us
  transfers between devices with their start and end apart: 8, of which 3 were waited for; matrix products, arithmetic and copies ran while one was open for 10% of the time, Pallas kernels for 0%

commit v1 on v0

v1 whole, which is shorter than its diff:
```python
import functools

import jax
import jax.numpy as jnp
from jax import lax
from jax.experimental import pallas as pl
from jax.experimental.pallas import tpu as pltpu
from jax.sharding import PartitionSpec as P

MESH = pl.DeviceIdType.MESH
LANES = 128
EARLY = 2


def kernel(
    nrow, nphi, rows, cells, cycles,
    widths, hydro, face, diffusion, conserved, faces_out,
    H, F, O, SL, SR, PL, PR, SF, RF, FN, M, MG, ELO, EHI, EL, ER,
    load_sem, out_sem, send_phi, recv_phi, send_mean, recv_mean, send_row, recv_row,
):
    nvar = hydro.shape[0]
    nface = face.shape[0]
    theta = hydro.shape[2]
    tiles = theta // LANES
    last = tiles - 1
    body = rows * cells
    row = lax.axis_index("row")
    phi = lax.axis_index("phi")
    left = lax.rem(phi + nphi - 1, nphi)
    right = lax.rem(phi + 1, nphi)
    packed = 2 * cycles

    loads = []
    for k in range(nvar):
        loads.append([pltpu.make_async_copy(
            hydro.at[k, :, pl.ds(t * LANES, LANES)], H.at[k, t, pl.ds(2 * cells, body)], load_sem.at[k, t])
            for t in range(tiles)])
    for k in range(nface):
        loads.append([pltpu.make_async_copy(
            face.at[k, :, pl.ds(t * LANES, LANES)], F.at[k, t], load_sem.at[nvar + k, t])
            for t in range(tiles)])
    for group in loads:
        for c in group:
            c.start()

    barrier = pltpu.get_barrier_semaphore()
    for step in range(1, nphi):
        pl.semaphore_signal(barrier, inc=1, device_id={"phi": lax.rem(phi + step, nphi)}, device_id_type=MESH)

    @pl.when(row > 0)
    def _():
        pl.semaphore_signal(barrier, inc=1, device_id={"row": row - 1}, device_id_type=MESH)

    @pl.when(row < nrow - 1)
    def _():
        pl.semaphore_signal(barrier, inc=1, device_id={"row": row + 1}, device_id_type=MESH)

    lane = lax.broadcasted_iota(jnp.int32, (1, LANES), 1)
    width_raw = jnp.zeros((1, LANES), jnp.int32)
    width_packed = jnp.zeros((1, LANES), jnp.int32)
    slot = lax.rem(lane, packed)
    for j in range(cycles):
        width_raw = jnp.where(lane == j, widths[j], width_raw)
        width_raw = jnp.where(lane == LANES - cycles + j, widths[cycles + j], width_raw)
        width_packed = jnp.where(slot == cycles + j, widths[j], width_packed)
        width_packed = jnp.where(slot == j, widths[cycles + j], width_packed)
    low = lane < cycles
    high = lane >= LANES - cycles

    def part(t):
        return slice(t * LANES, (t + 1) * LANES)

    def pack(value, f):
        return pltpu.roll(value, (cycles + packed * f) % LANES, 1)

    def unpack(value, f):
        return pltpu.roll(value, (-(cycles + packed * f)) % LANES, 1)

    def layer(ref, k, first, cell, t):
        return ref[k, t, pl.ds(first + cell, rows, stride=cells), :]

    def phi_copies(k):
        return (
            pltpu.make_async_remote_copy(
                src_ref=SL.at[k], dst_ref=PR.at[k], send_sem=send_phi.at[0, k], recv_sem=recv_phi.at[0, k],
                device_id={"phi": left}, device_id_type=MESH),
            pltpu.make_async_remote_copy(
                src_ref=SR.at[k], dst_ref=PL.at[k], send_sem=send_phi.at[1, k], recv_sem=recv_phi.at[1, k],
                device_id={"phi": right}, device_id_type=MESH),
        )

    def pack_halo(k):
        for t in range(tiles):
            for i in range(2):
                SL[k, i, :, part(t)] = layer(H, k, 2 * cells, i, t)
                SR[k, i, :, part(t)] = layer(H, k, 2 * cells, cells - 2 + i, t)

    for k in range(EARLY):
        for c in loads[k]:
            c.wait()
        pack_halo(k)

    peers = nphi - 1 + jnp.where(row > 0, 1, 0) + jnp.where(row < nrow - 1, 1, 0)
    pl.semaphore_wait(barrier, peers)
    for k in range(EARLY):
        for c in phi_copies(k):
            c.start()
    for k in range(EARLY, nvar + nface):
        for c in loads[k]:
            c.wait()

    for t in range(tiles):
        SF[:, part(t)] = layer(F, nface - 1, 0, 0, t)
    for k in range(EARLY, nvar):
        pack_halo(k)

    index = lax.broadcasted_iota(jnp.int32, (cells, LANES), 0)

    def local_average(r, carry):
        mean_row = jnp.zeros((1, LANES), jnp.float32)
        lo_row = jnp.zeros((1, LANES), jnp.float32)
        hi_row = jnp.zeros((1, LANES), jnp.float32)
        for f in range(nvar + nface):
            ref, k, base = (H, f, 2 * cells) if f < nvar else (F, f - nvar, 0)
            where = pl.ds(pl.multiple_of(base + r * cells, cells), cells)
            first = ref[k, 0, where, :]
            final = ref[k, last, where, :]
            total = jnp.where(low, first, final)
            result = total
            size = 1
            while size < cells:
                forward = pltpu.roll(total, cells - size, 0)
                if 2 * size < cells:
                    backward = pltpu.roll(total, size, 0)
                    forward = jnp.where((index & size) == 0, forward, backward)
                total = total + forward
                size *= 2
                result = jnp.where(width_raw == size, total * (1.0 / size), result)
            ref[k, 0, where, :] = jnp.where(low, result, first)
            second = result if last > 0 else jnp.where(low, result, final)
            keep = final if last > 0 else second
            ref[k, last, where, :] = jnp.where(high, result, keep)
            mine = (lane >= packed * f) & (lane < packed * (f + 1))
            mean_row = jnp.where(mine, pack(total[0:1] * (1.0 / cells), f), mean_row)
            lo_row = jnp.where(mine, pack(result[0:1], f), lo_row)
            hi_row = jnp.where(mine, pack(result[cells - 1 : cells], f), hi_row)
        M[pl.ds(r, 1), :] = mean_row
        ELO[pl.ds(r, 1), :] = lo_row
        EHI[pl.ds(r, 1), :] = hi_row
        return carry

    lax.fori_loop(0, rows, local_average, 0)

    def mean_copy(step):
        return pltpu.make_async_remote_copy(
            src_ref=M, dst_ref=MG.at[phi], send_sem=send_mean.at[step], recv_sem=recv_mean.at[step],
            device_id={"phi": lax.rem(phi + step, nphi)}, device_id_type=MESH)

    edge_left = pltpu.make_async_remote_copy(
        src_ref=ELO, dst_ref=ER, send_sem=send_phi.at[0, nvar], recv_sem=recv_phi.at[0, nvar],
        device_id={"phi": left}, device_id_type=MESH)
    edge_right = pltpu.make_async_remote_copy(
        src_ref=EHI, dst_ref=EL, send_sem=send_phi.at[1, nvar], recv_sem=recv_phi.at[1, nvar],
        device_id={"phi": right}, device_id_type=MESH)
    face_left = pltpu.make_async_remote_copy(
        src_ref=SF, dst_ref=RF, send_sem=send_phi.at[0, nvar + 1], recv_sem=recv_phi.at[0, nvar + 1],
        device_id={"phi": left}, device_id_type=MESH)
    for step in range(1, nphi):
        mean_copy(step).start()
    edge_left.start()
    edge_right.start()
    for k in range(EARLY, nvar):
        for c in phi_copies(k):
            c.start()
    face_left.start()

    MG[phi] = M[...]
    for step in range(1, nphi):
        mean_copy(step).wait_recv()

    def group_mean(who, initial):
        result = initial
        size = 2
        while size <= nphi:
            start = (who // size) * size
            total = MG[start]
            for i in range(1, size):
                total = total + MG[start + i]
            result = jnp.where(width_packed == size * cells, total * (1.0 / size), result)
            size *= 2
        return result

    M2 = group_mean(phi, M[...])
    ELO_next = group_mean(right, jnp.zeros_like(M2))
    EHI_next = group_mean(left, jnp.zeros_like(M2))
    MG[phi] = M2
    wide = width_raw > cells
    low_wide = low & wide
    high_wide = high & wide

    def wide_average(r):
        mean_row = MG[phi, pl.ds(r, 1), :]
        for f in range(nvar + nface):
            ref, k, base = (H, f, 2 * cells) if f < nvar else (F, f - nvar, 0)
            where = pl.ds(pl.multiple_of(base + r * cells, cells), cells)
            mean = jnp.broadcast_to(unpack(mean_row, f), (cells, LANES))
            ref[k, 0, where, :] = jnp.where(low_wide, mean, ref[k, 0, where, :])
            ref[k, last, where, :] = jnp.where(high_wide, mean, ref[k, last, where, :])

    for r in (0, 1, rows - 2, rows - 1):
        wide_average(r)

    lax.fori_loop(2, rows - 2, lambda r, c: (wide_average(r), c)[1], 0)

    down = pltpu.make_async_remote_copy(
        src_ref=H.at[:, :, pl.ds(2 * cells, 2 * cells)], dst_ref=H.at[:, :, pl.ds((rows + 2) * cells, 2 * cells)],
        send_sem=send_row.at[0], recv_sem=recv_row.at[0], device_id={"row": row - 1}, device_id_type=MESH)
    down_face = pltpu.make_async_remote_copy(
        src_ref=F.at[0, :, pl.ds(0, cells)], dst_ref=FN,
        send_sem=send_row.at[1], recv_sem=recv_row.at[1], device_id={"row": row - 1}, device_id_type=MESH)
    up = pltpu.make_async_remote_copy(
        src_ref=H.at[:, :, pl.ds(rows * cells, 2 * cells)], dst_ref=H.at[:, :, pl.ds(0, 2 * cells)],
        send_sem=send_row.at[2], recv_sem=recv_row.at[2], device_id={"row": row + 1}, device_id_type=MESH)

    @pl.when(row > 0)
    def _():
        down.start()
        down_face.start()

    @pl.when(row < nrow - 1)
    def _():
        up.start()

    faces_copies = [
        pltpu.make_async_copy(F.at[k, t], faces_out.at[k, :, pl.ds(t * LANES, LANES)], out_sem.at[nvar + nface + k, t])
        for k in range(nface) for t in range(tiles)]
    for c in faces_copies:
        c.start()

    @pl.when(row == 0)
    def _():
        H[:, :, pl.ds(0, 2 * cells), :] = jnp.zeros((nvar, tiles, 2 * cells, LANES), jnp.float32)

    @pl.when(row == nrow - 1)
    def _():
        H[:, :, pl.ds((rows + 2) * cells, 2 * cells), :] = jnp.zeros((nvar, tiles, 2 * cells, LANES), jnp.float32)
        FN[...] = jnp.zeros_like(FN)

    @pl.when(row > 0)
    def _():
        up.wait_recv()

    @pl.when(row < nrow - 1)
    def _():
        down.wait_recv()
        down_face.wait_recv()

    def shifted(parts, amount):
        out = []
        turned = [pltpu.roll(p, (-amount) % LANES, 1) for p in parts]
        for t in range(tiles):
            if amount > 0:
                inside = lane < LANES - amount
                other = turned[t + 1] if t + 1 < tiles else 0.0
            else:
                inside = lane >= -amount
                other = turned[t - 1] if t > 0 else 0.0
            out.append(jnp.where(inside, turned[t], other))
        return out

    def smooth_row(r, carry):
        for k in range(nvar):
            def at(offset, t):
                return H[k, t, pl.ds(pl.multiple_of((r + 2 + offset) * cells, cells), cells), :]
            mid = [at(0, t) for t in range(tiles)]
            one = [a + b for a, b in zip(shifted(mid, 1), shifted(mid, -1))]
            two = [a + b for a, b in zip(shifted(mid, 2), shifted(mid, -2))]
            for t in range(tiles):
                v = mid[t]
                s1 = one[t] + (pltpu.roll(v, 1, 0) + pltpu.roll(v, cells - 1, 0)) + (at(-1, t) + at(1, t))
                s2 = two[t] + (pltpu.roll(v, 2, 0) + pltpu.roll(v, cells - 2, 0)) + (at(-2, t) + at(2, t))
                change = (16.0 * s1 - s2 - 90.0 * v) * (1.0 / 12.0)
                O[k, t, pl.ds(pl.multiple_of(r * cells, cells), cells), :] = v + diffusion[k : k + 1, part(t)] * change
        return carry

    def field_row(r, following):
        here = pl.ds(pl.multiple_of(r * cells, cells), cells)
        polar = [F[1, t, here, :] for t in range(tiles)]
        polar_next = shifted(polar, 1)
        for t in range(tiles):
            O[nvar, t, here, :] = 0.5 * (F[0, t, here, :] + following(t))
            O[nvar + 1, t, here, :] = 0.5 * (polar[t] + polar_next[t])
            azimuth = F[2, t, here, :]
            O[nvar + 2, t, here, :] = 0.5 * (azimuth + pltpu.roll(azimuth, cells - 1, 0))

    def field_loop(r, carry):
        field_row(r, lambda t: F[0, t, pl.ds(pl.multiple_of((r + 1) * cells, cells), cells), :])
        return carry

    lax.fori_loop(0, rows - 1, field_loop, 0)
    field_row(rows - 1, lambda t: FN[t])
    outs = [[
        pltpu.make_async_copy(O.at[k, t], conserved.at[k, :, pl.ds(t * LANES, LANES)], out_sem.at[k, t])
        for t in range(tiles)] for k in range(nvar + nface)]

    def store(k):
        for c in outs[k]:
            c.start()

    store(nvar)
    store(nvar + 1)
    lax.fori_loop(0, rows, smooth_row, 0)

    edge_left.wait_recv()
    edge_right.wait_recv()
    local = width_packed <= cells
    from_left = jnp.where(local, EL[...], EHI_next)
    from_right = jnp.where(local, ER[...], ELO_next)

    def fixed(raw, edge, t):
        if t == 0:
            raw = jnp.where(low, edge, raw)
        if t == last:
            raw = jnp.where(high, edge, raw)
        return raw

    for k in range(nvar):
        for c in phi_copies(k):
            c.wait_recv()
        edge_l = unpack(from_left, k)
        edge_r = unpack(from_right, k)
        for t in range(tiles):
            scale = diffusion[k : k + 1, part(t)] * (1.0 / 12.0)
            l1 = fixed(PL[k, 1, :, part(t)], edge_l, t) - layer(H, k, 2 * cells, cells - 1, t)
            l2 = fixed(PL[k, 0, :, part(t)], edge_l, t) - layer(H, k, 2 * cells, cells - 2, t)
            r1 = fixed(PR[k, 0, :, part(t)], edge_r, t) - layer(H, k, 2 * cells, 0, t)
            r2 = fixed(PR[k, 1, :, part(t)], edge_r, t) - layer(H, k, 2 * cells, 1, t)
            for cell, term in ((0, 16.0 * l1 - l2), (1, -l1), (cells - 2, -r1), (cells - 1, 16.0 * r1 - r2)):
                spot = pl.ds(cell, rows, stride=cells)
                O[k, t, spot, :] = O[k, t, spot, :] + scale * term
        store(k)

    face_left.wait_recv()
    edge_f = unpack(from_right, nvar + nface - 1)
    for t in range(tiles):
        spot = pl.ds(cells - 1, rows, stride=cells)
        O[nvar + 2, t, spot, :] = 0.5 * (layer(F, nface - 1, 0, cells - 1, t) + fixed(RF[:, part(t)], edge_f, t))
    store(nvar + 2)

    for k in range(nvar):
        for c in phi_copies(k):
            c.wait_send()
    edge_left.wait_send()
    edge_right.wait_send()
    face_left.wait_send()
    for step in range(1, nphi):
        mean_copy(step).wait_send()

    @pl.when(row > 0)
    def _():
        down.wait_send()
        down_face.wait_send()

    @pl.when(row < nrow - 1)
    def _():
        up.wait_send()

    for c in faces_copies:
        c.wait()
    for group in outs:
        for c in group:
            c.wait()


def body(nrow, nphi, hydro_vars, face_b, widths, diffusion):
    nvar, rows, cells, theta = hydro_vars.shape
    nface = face_b.shape[0]
    cycles = widths.shape[0] // 2
    f32 = jnp.float32
    tiles = theta // LANES
    shape = lambda *s: pltpu.VMEM(s, f32)
    anywhere = pl.BlockSpec(memory_space=pl.ANY)
    conserved, faces = pl.pallas_call(
        functools.partial(kernel, nrow, nphi, rows, cells, cycles),
        out_shape=(
            jax.ShapeDtypeStruct((nvar + nface, rows * cells, theta), f32),
            jax.ShapeDtypeStruct((nface, rows * cells, theta), f32),
        ),
        in_specs=[
            pl.BlockSpec(memory_space=pltpu.SMEM),
            anywhere,
            anywhere,
            pl.BlockSpec(memory_space=pltpu.VMEM),
        ],
        out_specs=(anywhere, anywhere),
        scratch_shapes=[
            shape(nvar, tiles, (rows + 4) * cells, LANES),
            shape(nface, tiles, rows * cells, LANES),
            shape(nvar + nface, tiles, rows * cells, LANES),
            shape(nvar, 2, rows, theta),
            shape(nvar, 2, rows, theta),
            shape(nvar, 2, rows, theta),
            shape(nvar, 2, rows, theta),
            shape(rows, theta),
            shape(rows, theta),
            shape(tiles, cells, LANES),
            shape(rows, LANES),
            shape(nphi, rows, LANES),
            shape(rows, LANES),
            shape(rows, LANES),
            shape(rows, LANES),
            shape(rows, LANES),
            pltpu.SemaphoreType.DMA((nvar + nface, tiles)),
            pltpu.SemaphoreType.DMA((nvar + 2 * nface, tiles)),
            pltpu.SemaphoreType.DMA((2, nvar + 2)),
            pltpu.SemaphoreType.DMA((2, nvar + 2)),
            pltpu.SemaphoreType.DMA((nphi,)),
            pltpu.SemaphoreType.DMA((nphi,)),
            pltpu.SemaphoreType.DMA((3,)),
            pltpu.SemaphoreType.DMA((3,)),
        ],
        compiler_params=pltpu.CompilerParams(
            collective_id=0, has_side_effects=True, vmem_limit_bytes=40 * 1024 * 1024
        ),
        name="step",
    )(
        widths,
        hydro_vars.reshape(nvar, rows * cells, theta),
        face_b.reshape(nface, rows * cells, theta),
        diffusion,
    )
    return (
        conserved.reshape(nvar + nface, rows, cells, theta),
        faces.reshape(nface, rows, cells, theta),
    )


def solution(mesh):
    spec = P(None, "row", "phi", None)
    return jax.shard_map(
        functools.partial(body, mesh.shape["row"], mesh.shape["phi"]),
        mesh=mesh,
        in_specs=(spec, spec, P(), P()),
        out_specs=(spec, spec),
        check_vma=False,
    )
```

time: 85 us -> 44.6 us (0.52)
  the two profiles are of different devices: /device:TPU:0 before, /device:TPU:1 now
where the time goes in v1:
time: 44.6 us; the launch traced here: 44.4 us
  Pallas kernels  36.1 us (81%)
  local copies, waits for them, and re-layouts  7.65 us (17%)
  between operations  0.65 us (1%)
    pallas_call x1, Pallas kernels, body(): pl.pallas_call(functools.partial(kernel, nrow, nphi, rows, cells, cycles)...  36.1 us
    unnamed x10, local copies, waits for them, and re-layouts  7.65 us

profile of v1, /device:TPU:1, one launch (start us, length us, event | category | flops | bytes accessed | tf_op | source)
XLA Modules:
  0.0 44.4 jit_solution(10425558071586348164)
XLA Ops:
  0.6 0.0 copy-start
  0.6 1.7 %copy-done = f32[5,32,16,256]{3,2,1,0:T(8,128)S(1)} copy-done((f32[5,32,16,256]{3,2,1,0:T(8,128)S(1)}, f32[5,32,16,256]{3,2,1,0:T(8,128)}, u32[]{:S(2)}) %copy-start) | copy-done | bytes 2621464
  2.4 0.0 copy-start.1
  2.4 1.4 %copy-done.1 = f32[3,32,16,256]{3,2,1,0:T(8,128)S(1)} copy-done((f32[3,32,16,256]{3,2,1,0:T(8,128)S(1)}, f32[3,32,16,256]{3,2,1,0:T(8,128)}, u32[]{:S(2)}) %copy-start.1) | copy-done | bytes 1572888
  3.8 0.0 copy-start.2
  3.8 0.7 %copy-done.2 = f32[5,256]{1,0:T(8,128)S(1)} copy-done((f32[5,256]{1,0:T(8,128)S(1)}, f32[5,256]{1,0:T(8,128)}, u32[]{:S(2)}) %copy-start.2) | copy-done | bytes 5144
  4.5 0.0 copy-start.3
  4.5 0.7 %copy-done.3 = s32[16]{0:T(128)S(1)} copy-done((s32[16]{0:T(128)S(1)}, s32[16]{0:T(128)}, u32[]{:S(2)}) %copy-start.3) | copy-done | bytes 88
  5.1 36.1 %step.1 = (f32[8,512,256]{2,1,0:T(8,128)S(1)}, f32[3,512,256]{2,1,0:T(8,128)S(1)}) custom-call(s32[16]{0:T(128)S(1)} %copy-done.3, f32[5,512,256]{2,1,0:T(8,128)S(1)} %bitcast.5, f32[3,512,256]{2,1,0:T(8,128)S(1)} %bitcast.6, f32[5,256]{1,0:T(8,128)S(1)} %copy-done.2), custom_call_target="tpu_custom_call" | custom-call | tf_op jit(solution)/shard_map/step/pallas_call | solution.py:383
  41.2 2.0 %copy.8 = f32[8,32,16,256]{3,2,1,0:T(8,128)} copy(f32[8,32,16,256]{3,2,1,0:T(8,128)S(1)} %bitcast.4) | data formatting | bytes 8388608
  43.3 1.1 %copy.9 = f32[3,32,16,256]{3,2,1,0:T(8,128)} copy(f32[3,32,16,256]{3,2,1,0:T(8,128)S(1)} %bitcast.7) | data formatting | bytes 3145728
Async XLA Ops:
  0.6 1.7 %copy-start = (f32[5,32,16,256]{3,2,1,0:T(8,128)S(1)}, f32[5,32,16,256]{3,2,1,0:T(8,128)}, u32[]{:S(2)}) copy-start(f32[5,32,16,256]{3,2,1,0:T(8,128)} %param.4) | copy-start | bytes 7864324
  2.4 1.4 %copy-start.1 = (f32[3,32,16,256]{3,2,1,0:T(8,128)S(1)}, f32[3,32,16,256]{3,2,1,0:T(8,128)}, u32[]{:S(2)}) copy-start(f32[3,32,16,256]{3,2,1,0:T(8,128)} %param.5) | copy-start | bytes 4718596
  3.8 0.7 %copy-start.2 = (f32[5,256]{1,0:T(8,128)S(1)}, f32[5,256]{1,0:T(8,128)}, u32[]{:S(2)}) copy-start(f32[5,256]{1,0:T(8,128)} %diffusion.1) | copy-start | bytes 15364
  4.5 0.7 %copy-start.3 = (s32[16]{0:T(128)S(1)}, s32[16]{0:T(128)}, u32[]{:S(2)}) copy-start(s32[16]{0:T(128)} %widths.1) | copy-start | bytes 196

commit v2 on v1

v2 whole, which is shorter than its diff:
```python
import functools

import jax
import jax.numpy as jnp
from jax import lax
from jax.experimental import pallas as pl
from jax.experimental.pallas import tpu as pltpu
from jax.sharding import PartitionSpec as P

MESH = pl.DeviceIdType.MESH
LANES = 128
SUB = 8
EARLY = 1
LIMIT = 67000000


def kernel(
    nrow, nphi, rows, cells, tiles, cycles,
    widths_far, hydro, face, diffusion_far, O, F,
    H, SL, SR, PL, PR, SF, RF, FN, Q, M, MG, ELO, EHI, EL, ER,
    widths, diffusion, small_sem, load_sem, send_phi, recv_phi, send_mean, recv_mean, send_row, recv_row,
):
    nvar = hydro.shape[0]
    nface = face.shape[0]
    fields = nvar + nface
    last = tiles - 1
    blocks = cells // SUB
    ring = cells * tiles
    row = lax.axis_index("row")
    phi = lax.axis_index("phi")
    left = lax.rem(phi + nphi - 1, nphi)
    right = lax.rem(phi + 1, nphi)
    packed = 2 * cycles

    loads = [pltpu.make_async_copy(hydro.at[k], H.at[k, pl.ds(2 * ring, rows * ring)], load_sem.at[k]) for k in range(nvar)]
    loads += [pltpu.make_async_copy(face.at[k], F.at[k], load_sem.at[nvar + k]) for k in range(nface)]
    small = [
        pltpu.make_async_copy(widths_far, widths, small_sem.at[0]),
        pltpu.make_async_copy(diffusion_far, diffusion, small_sem.at[1]),
    ]
    for c in small + loads:
        c.start()

    barrier = pltpu.get_barrier_semaphore()
    for step in range(1, nphi):
        pl.semaphore_signal(barrier, inc=1, device_id={"phi": lax.rem(phi + step, nphi)}, device_id_type=MESH)

    @pl.when(row > 0)
    def _():
        pl.semaphore_signal(barrier, inc=1, device_id={"row": row - 1}, device_id_type=MESH)

    @pl.when(row < nrow - 1)
    def _():
        pl.semaphore_signal(barrier, inc=1, device_id={"row": row + 1}, device_id_type=MESH)

    for c in small:
        c.wait()
    lane = lax.broadcasted_iota(jnp.int32, (1, LANES), 1)
    width = jnp.zeros((1, LANES), jnp.int32)
    slot = lax.rem(lane, packed)
    for j in range(cycles):
        width = jnp.where(slot == cycles + j, widths[j], width)
        width = jnp.where(slot == j, widths[cycles + j], width)
    low = lane < cycles
    high = lane >= LANES - cycles
    mine = [(lane >= packed * f) & (lane < packed * (f + 1)) for f in range(fields)]

    def part(t):
        return slice(t * LANES, (t + 1) * LANES)

    def pack(value, f):
        return pltpu.roll(value, (cycles + packed * f) % LANES, 1)

    def unpack(value, f):
        return pltpu.roll(value, (-(cycles + packed * f)) % LANES, 1)

    def spot(r, b, t):
        start = r * ring + (b * tiles + t) * SUB
        return pl.ds(start if isinstance(r, int) else pl.multiple_of(start, SUB), SUB)

    def layer(r, cell, t):
        return pl.ds(r * ring + (cell // SUB * tiles + t) * SUB + cell % SUB, rows, stride=ring)

    def place(f):
        return (H, f, 2) if f < nvar else (F, f - nvar, 0)

    def phi_copies(k):
        return (
            pltpu.make_async_remote_copy(
                src_ref=SL.at[k], dst_ref=PR.at[k], send_sem=send_phi.at[0, k], recv_sem=recv_phi.at[0, k],
                device_id={"phi": left}, device_id_type=MESH),
            pltpu.make_async_remote_copy(
                src_ref=SR.at[k], dst_ref=PL.at[k], send_sem=send_phi.at[1, k], recv_sem=recv_phi.at[1, k],
                device_id={"phi": right}, device_id_type=MESH),
        )

    def pack_halo(k):
        for t in range(tiles):
            for i in range(2):
                SL[k, i, t] = H[k, layer(2, i, t), :]
                SR[k, i, t] = H[k, layer(2, cells - 2 + i, t), :]

    for k in range(EARLY):
        loads[k].wait()
        pack_halo(k)
    peers = nphi - 1 + jnp.where(row > 0, 1, 0) + jnp.where(row < nrow - 1, 1, 0)
    pl.semaphore_wait(barrier, peers)
    for k in range(EARLY):
        for c in phi_copies(k):
            c.start()
    for k in range(EARLY, fields):
        loads[k].wait()

    index = lax.broadcasted_iota(jnp.int32, (SUB, LANES), 0)

    def local_average(r, carry):
        totals = []
        for b in range(blocks):
            value = jnp.zeros((SUB, LANES), jnp.float32)
            for f in range(fields):
                ref, k, base = place(f)
                polar = jnp.where(low, ref[k, spot(r + base, b, 0), :], ref[k, spot(r + base, b, last), :])
                value = jnp.where(mine[f], pack(polar, f), value)
            totals.append(value)
        results = list(totals)
        size = 1
        while size < cells:
            if size < SUB:
                turned = []
                for v in totals:
                    forward = pltpu.roll(v, SUB - size, 0)
                    if 2 * size < SUB:
                        forward = jnp.where((index & size) == 0, forward, pltpu.roll(v, size, 0))
                    turned.append(v + forward)
                totals = turned
            else:
                hop = size // SUB
                totals = [totals[b] + totals[b ^ hop] for b in range(blocks)]
            size *= 2
            results = [jnp.where(width == size, v * (1.0 / size), old) for v, old in zip(totals, results)]
        for b in range(blocks):
            Q[pl.ds(pl.multiple_of(r * cells + b * SUB, SUB), SUB), :] = results[b]
        M[pl.ds(r, 1), :] = totals[0][0:1] * (1.0 / cells)
        ELO[pl.ds(r, 1), :] = results[0][0:1]
        EHI[pl.ds(r, 1), :] = results[blocks - 1][SUB - 1 : SUB]
        return carry

    lax.fori_loop(0, rows, local_average, 0)

    def mean_copy(step):
        return pltpu.make_async_remote_copy(
            src_ref=M, dst_ref=MG.at[phi], send_sem=send_mean.at[step], recv_sem=recv_mean.at[step],
            device_id={"phi": lax.rem(phi + step, nphi)}, device_id_type=MESH)

    edge_left = pltpu.make_async_remote_copy(
        src_ref=ELO, dst_ref=ER, send_sem=send_phi.at[0, nvar], recv_sem=recv_phi.at[0, nvar],
        device_id={"phi": left}, device_id_type=MESH)
    edge_right = pltpu.make_async_remote_copy(
        src_ref=EHI, dst_ref=EL, send_sem=send_phi.at[1, nvar], recv_sem=recv_phi.at[1, nvar],
        device_id={"phi": right}, device_id_type=MESH)
    face_left = pltpu.make_async_remote_copy(
        src_ref=SF, dst_ref=RF, send_sem=send_phi.at[0, nvar + 1], recv_sem=recv_phi.at[0, nvar + 1],
        device_id={"phi": left}, device_id_type=MESH)
    for step in range(1, nphi):
        mean_copy(step).start()
    edge_left.start()
    edge_right.start()
    for t in range(tiles):
        SF[t] = F[nface - 1, layer(0, 0, t), :]
    for k in range(EARLY, nvar):
        pack_halo(k)
    for k in range(EARLY, nvar):
        for c in phi_copies(k):
            c.start()
    face_left.start()

    MG[phi] = M[...]
    for step in range(1, nphi):
        mean_copy(step).wait_recv()

    def group_mean(who, initial):
        result = initial
        size = 2
        while size <= nphi:
            start = (who // size) * size
            total = MG[start]
            for i in range(1, size):
                total = total + MG[start + i]
            result = jnp.where(width == size * cells, total * (1.0 / size), result)
            size *= 2
        return result

    own_mean = group_mean(phi, M[...])
    next_lo = group_mean(right, jnp.zeros_like(own_mean))
    next_hi = group_mean(left, jnp.zeros_like(own_mean))
    MG[phi] = own_mean
    wide = width > cells

    def spread(r):
        mean = jnp.broadcast_to(MG[phi, pl.ds(r, 1), :], (SUB, LANES))
        for b in range(blocks):
            where = pl.ds(r * cells + b * SUB if isinstance(r, int) else pl.multiple_of(r * cells + b * SUB, SUB), SUB)
            value = jnp.where(wide, mean, Q[where, :])
            for f in range(fields):
                ref, k, base = place(f)
                polar = unpack(value, f)
                ref[k, spot(r + base, b, 0), :] = jnp.where(low, polar, ref[k, spot(r + base, b, 0), :])
                ref[k, spot(r + base, b, last), :] = jnp.where(high, polar, ref[k, spot(r + base, b, last), :])

    for r in (0, 1, rows - 2, rows - 1):
        spread(r)
    lax.fori_loop(2, rows - 2, lambda r, c: (spread(r), c)[1], 0)

    down = pltpu.make_async_remote_copy(
        src_ref=H.at[:, pl.ds(2 * ring, 2 * ring)], dst_ref=H.at[:, pl.ds((rows + 2) * ring, 2 * ring)],
        send_sem=send_row.at[0], recv_sem=recv_row.at[0], device_id={"row": row - 1}, device_id_type=MESH)
    down_face = pltpu.make_async_remote_copy(
        src_ref=F.at[0, pl.ds(0, ring)], dst_ref=FN,
        send_sem=send_row.at[1], recv_sem=recv_row.at[1], device_id={"row": row - 1}, device_id_type=MESH)
    up = pltpu.make_async_remote_copy(
        src_ref=H.at[:, pl.ds(rows * ring, 2 * ring)], dst_ref=H.at[:, pl.ds(0, 2 * ring)],
        send_sem=send_row.at[2], recv_sem=recv_row.at[2], device_id={"row": row + 1}, device_id_type=MESH)

    @pl.when(row > 0)
    def _():
        down.start()
        down_face.start()

    @pl.when(row < nrow - 1)
    def _():
        up.start()

    @pl.when(row == 0)
    def _():
        H[:, pl.ds(0, 2 * ring), :] = jnp.zeros((nvar, 2 * ring, LANES), jnp.float32)

    @pl.when(row == nrow - 1)
    def _():
        H[:, pl.ds((rows + 2) * ring, 2 * ring), :] = jnp.zeros((nvar, 2 * ring, LANES), jnp.float32)
        FN[...] = jnp.zeros_like(FN)

    def whole(ref, k, r, t):
        return jnp.concatenate([ref[k, spot(r, b, t), :] for b in range(blocks)], 0)

    def write(k, r, t, value):
        for b in range(blocks):
            O[k, spot(r, b, t), :] = value[b * SUB : (b + 1) * SUB]

    def shifted(parts, amount):
        out = []
        turned = [pltpu.roll(p, (-amount) % LANES, 1) for p in parts]
        for t in range(tiles):
            if amount > 0:
                inside = lane < LANES - amount
                other = turned[t + 1] if t + 1 < tiles else 0.0
            else:
                inside = lane >= -amount
                other = turned[t - 1] if t > 0 else 0.0
            out.append(jnp.where(inside, turned[t], other))
        return out

    def smooth_row(r):
        for k in range(nvar):
            mid = [whole(H, k, r + 2, t) for t in range(tiles)]
            one = [a + b for a, b in zip(shifted(mid, 1), shifted(mid, -1))]
            two = [a + b for a, b in zip(shifted(mid, 2), shifted(mid, -2))]
            for t in range(tiles):
                v = mid[t]
                s1 = one[t] + (pltpu.roll(v, 1, 0) + pltpu.roll(v, cells - 1, 0)) + (whole(H, k, r + 1, t) + whole(H, k, r + 3, t))
                s2 = two[t] + (pltpu.roll(v, 2, 0) + pltpu.roll(v, cells - 2, 0)) + (whole(H, k, r, t) + whole(H, k, r + 4, t))
                change = (16.0 * s1 - s2 - 90.0 * v) * (1.0 / 12.0)
                write(k, r, t, v + diffusion[k : k + 1, part(t)] * change)

    def field_row(r, following):
        polar = [whole(F, 1, r, t) for t in range(tiles)]
        polar_next = shifted(polar, 1)
        for t in range(tiles):
            write(nvar, r, t, 0.5 * (whole(F, 0, r, t) + following(t)))
            write(nvar + 1, r, t, 0.5 * (polar[t] + polar_next[t]))
            azimuth = whole(F, 2, r, t)
            write(nvar + 2, r, t, 0.5 * (azimuth + pltpu.roll(azimuth, cells - 1, 0)))

    def inner_row(r, carry):
        field_row(r, lambda t: whole(F, 0, r + 1, t))
        smooth_row(r)
        return carry

    lax.fori_loop(2, rows - 2, inner_row, 0)
    for r in (0, 1, rows - 2):
        field_row(r, lambda t, r=r: whole(F, 0, r + 1, t))

    @pl.when(row > 0)
    def _():
        up.wait_recv()

    @pl.when(row < nrow - 1)
    def _():
        down.wait_recv()
        down_face.wait_recv()

    field_row(rows - 1, lambda t: jnp.concatenate([FN[spot(0, b, t), :] for b in range(blocks)], 0))
    for r in (0, 1, rows - 2, rows - 1):
        smooth_row(r)

    edge_left.wait_recv()
    edge_right.wait_recv()
    local = width <= cells
    from_left = jnp.where(local, EL[...], next_hi)
    from_right = jnp.where(local, ER[...], next_lo)

    def fixed(raw, edge, t):
        if t == 0:
            raw = jnp.where(low, edge, raw)
        if t == last:
            raw = jnp.where(high, edge, raw)
        return raw

    for k in range(nvar):
        for c in phi_copies(k):
            c.wait_recv()
        edge_l = unpack(from_left, k)
        edge_r = unpack(from_right, k)
        for t in range(tiles):
            scale = diffusion[k : k + 1, part(t)] * (1.0 / 12.0)
            l1 = fixed(PL[k, 1, t], edge_l, t) - H[k, layer(2, cells - 1, t), :]
            l2 = fixed(PL[k, 0, t], edge_l, t) - H[k, layer(2, cells - 2, t), :]
            r1 = fixed(PR[k, 0, t], edge_r, t) - H[k, layer(2, 0, t), :]
            r2 = fixed(PR[k, 1, t], edge_r, t) - H[k, layer(2, 1, t), :]
            for cell, term in ((0, 16.0 * l1 - l2), (1, -l1), (cells - 2, -r1), (cells - 1, 16.0 * r1 - r2)):
                O[k, layer(0, cell, t), :] = O[k, layer(0, cell, t), :] + scale * term

    face_left.wait_recv()
    edge_f = unpack(from_right, fields - 1)
    for t in range(tiles):
        O[fields - 1, layer(0, cells - 1, t), :] = 0.5 * (F[nface - 1, layer(0, cells - 1, t), :] + fixed(RF[t], edge_f, t))

    for k in range(nvar):
        for c in phi_copies(k):
            c.wait_send()
    edge_left.wait_send()
    edge_right.wait_send()
    face_left.wait_send()
    for step in range(1, nphi):
        mean_copy(step).wait_send()

    @pl.when(row > 0)
    def _():
        down.wait_send()
        down_face.wait_send()

    @pl.when(row < nrow - 1)
    def _():
        up.wait_send()


def blocked(x):
    n, rows, cells, theta = x.shape
    x = x.reshape(n, rows, cells // SUB, SUB, theta // LANES, LANES)
    return x.transpose(0, 1, 2, 4, 3, 5).reshape(n, rows * cells * (theta // LANES), LANES)


def unblocked(x, rows, cells, theta):
    x = x.reshape(x.shape[0], rows, cells // SUB, theta // LANES, SUB, LANES)
    return x.transpose(0, 1, 2, 4, 3, 5).reshape(x.shape[0], rows, cells, theta)


def body(nrow, nphi, hydro_vars, face_b, widths, diffusion):
    nvar, rows, cells, theta = hydro_vars.shape
    nface = face_b.shape[0]
    fields = nvar + nface
    cycles = widths.shape[0] // 2
    tiles = theta // LANES
    ring = cells * tiles
    f32 = jnp.float32
    shape = lambda *s: pltpu.VMEM(s, f32)
    far = pl.BlockSpec(memory_space=pltpu.HBM)
    near = pl.BlockSpec(memory_space=pltpu.VMEM)
    result_bytes = (fields + nface) * rows * ring * LANES * 4
    conserved, faces = pl.pallas_call(
        functools.partial(kernel, nrow, nphi, rows, cells, tiles, cycles),
        out_shape=(
            jax.ShapeDtypeStruct((fields, rows * ring, LANES), f32),
            jax.ShapeDtypeStruct((nface, rows * ring, LANES), f32),
        ),
        in_specs=[far, far, far, far],
        out_specs=(near, near),
        scratch_shapes=[
            shape(nvar, (rows + 4) * ring, LANES),
            shape(nvar, 2, tiles, rows, LANES),
            shape(nvar, 2, tiles, rows, LANES),
            shape(nvar, 2, tiles, rows, LANES),
            shape(nvar, 2, tiles, rows, LANES),
            shape(tiles, rows, LANES),
            shape(tiles, rows, LANES),
            shape(ring, LANES),
            shape(rows * cells, LANES),
            shape(rows, LANES),
            shape(nphi, rows, LANES),
            shape(rows, LANES),
            shape(rows, LANES),
            shape(rows, LANES),
            shape(rows, LANES),
            pltpu.SMEM((2 * cycles,), jnp.int32),
            shape(nvar, theta),
            pltpu.SemaphoreType.DMA((2,)),
            pltpu.SemaphoreType.DMA((fields,)),
            pltpu.SemaphoreType.DMA((2, nvar + 2)),
            pltpu.SemaphoreType.DMA((2, nvar + 2)),
            pltpu.SemaphoreType.DMA((nphi,)),
            pltpu.SemaphoreType.DMA((nphi,)),
            pltpu.SemaphoreType.DMA((3,)),
            pltpu.SemaphoreType.DMA((3,)),
        ],
        compiler_params=pltpu.CompilerParams(
            collective_id=0, has_side_effects=True, vmem_limit_bytes=LIMIT - result_bytes
        ),
        name="step",
    )(widths, blocked(hydro_vars), blocked(face_b), diffusion)
    return unblocked(conserved, rows, cells, theta), unblocked(faces, rows, cells, theta)


def solution(mesh):
    spec = P(None, "row", "phi", None)
    return jax.shard_map(
        functools.partial(body, mesh.shape["row"], mesh.shape["phi"]),
        mesh=mesh,
        in_specs=(spec, spec, P(), P()),
        out_specs=(spec, spec),
        check_vma=False,
    )
```

time: 44.6 us -> 36.6 us (0.82)
  the two profiles are of different devices: /device:TPU:1 before, /device:TPU:27 now
where the time goes in v2:
time: 36.6 us; the launch traced here: 36.4 us
  Pallas kernels  29.8 us (81%)
  local copies, waits for them, and re-layouts  5.91 us (16%)
  between operations  0.65 us (2%)
    pallas_call x1, Pallas kernels, body(): pl.pallas_call(functools.partial(kernel, nrow, nphi, rows, cells, tiles,...  29.8 us
    unnamed x4, local copies, waits for them, and re-layouts  5.91 us

profile of v2, /device:TPU:27, one launch (start us, length us, event | category | flops | bytes accessed | tf_op | source)
XLA Modules:
  0.0 36.4 jit_solution(16534503807190012614)
XLA Ops:
  0.6 29.8 %step.1 = (f32[8,1024,128]{2,1,0:T(8,128)}, f32[3,1024,128]{2,1,0:T(8,128)}) custom-call(s32[16]{0:T(128)} %widths_far.1, f32[5,1024,128]{2,1,0:T(8,128)} %bitcast.21, f32[3,1024,128]{2,1,0:T(8,128)} %bitcast.22, f32[5,256]{1,0:T(8,128)} %diffusion_far.1), custom_call_target="tpu_custom_call" | custom-call | tf_op jit(solution)/shard_map/step/pallas_call | solution.py:379
  30.5 0.0 copy-start
  30.5 4.8 %copy.8 = f32[8,32,16,256]{3,2,1,0:T(8,128)} copy(f32[8,32,16,256]{3,2,1,0:T(8,128)} %bitcast.20) | data formatting | bytes 8388608
  35.3 0.0 copy-done
  35.3 1.1 %copy.9 = f32[3,32,16,256]{3,2,1,0:T(8,128)} copy(f32[3,32,16,256]{3,2,1,0:T(8,128)S(1)} %bitcast.23) | data formatting | bytes 3145728
Async XLA Ops:
  30.5 4.8 %copy-start = (f32[3,1024,128]{2,1,0:T(8,128)S(1)}, f32[3,1024,128]{2,1,0:T(8,128)}, u32[]{:S(2)}) copy-start(f32[3,1024,128]{2,1,0:T(8,128)} %get-tuple-element.5) | copy-start | bytes 4718596

commit v3 on v2

--- a/solution.py
+++ b/solution.py
@@ -10,8 +10,8 @@
 MESH = pl.DeviceIdType.MESH
 LANES = 128
 SUB = 8
-EARLY = 1
-LIMIT = 67000000
+EARLY = 2
+LIMIT = 58000000
 
 
 def kernel(
@@ -94,34 +94,57 @@
                 device_id={"phi": right}, device_id_type=MESH),
         )
 
+    def mean_copy(step):
+        return pltpu.make_async_remote_copy(
+            src_ref=M, dst_ref=MG.at[phi], send_sem=send_mean.at[step], recv_sem=recv_mean.at[step],
+            device_id={"phi": lax.rem(phi + step, nphi)}, device_id_type=MESH)
+
     def pack_halo(k):
         for t in range(tiles):
             for i in range(2):
                 SL[k, i, t] = H[k, layer(2, i, t), :]
                 SR[k, i, t] = H[k, layer(2, cells - 2 + i, t), :]
 
-    for k in range(EARLY):
-        loads[k].wait()
-        pack_halo(k)
+    for c in loads:
+        c.wait()
+
+    def polar_cells(r, b):
+        value = jnp.zeros((SUB, LANES), jnp.float32)
+        for f in range(fields):
+            ref, k, base = place(f)
+            polar = jnp.where(low, ref[k, spot(r + base, b, 0), :], ref[k, spot(r + base, b, last), :])
+            value = jnp.where(mine[f], pack(polar, f), value)
+        return value
+
+    def cell_mean(r, carry):
+        value = jnp.zeros((SUB, LANES), jnp.float32)
+        for f in range(fields):
+            ref, k, base = place(f)
+            sums = [ref[k, spot(r + base, 0, t), :] for t in (0, last)]
+            for b in range(1, blocks):
+                sums = [x + ref[k, spot(r + base, b, t), :] for x, t in zip(sums, (0, last))]
+            value = jnp.where(mine[f], pack(jnp.where(low, sums[0], sums[1]), f), value)
+        size = SUB // 2
+        while size:
+            value = value + pltpu.roll(value, size, 0)
+            size //= 2
+        M[pl.ds(r, 1), :] = value[0:1] * (1.0 / cells)
+        return carry
+
+    lax.fori_loop(0, rows, cell_mean, 0, unroll=2)
     peers = nphi - 1 + jnp.where(row > 0, 1, 0) + jnp.where(row < nrow - 1, 1, 0)
     pl.semaphore_wait(barrier, peers)
+    for step in range(1, nphi):
+        mean_copy(step).start()
     for k in range(EARLY):
+        pack_halo(k)
         for c in phi_copies(k):
             c.start()
-    for k in range(EARLY, fields):
-        loads[k].wait()
 
     index = lax.broadcasted_iota(jnp.int32, (SUB, LANES), 0)
 
     def local_average(r, carry):
-        totals = []
-        for b in range(blocks):
-            value = jnp.zeros((SUB, LANES), jnp.float32)
-            for f in range(fields):
-                ref, k, base = place(f)
-                polar = jnp.where(low, ref[k, spot(r + base, b, 0), :], ref[k, spot(r + base, b, last), :])
-                value = jnp.where(mine[f], pack(polar, f), value)
-            totals.append(value)
+        totals = [polar_cells(r, b) for b in range(blocks)]
         results = list(totals)
         size = 1
         while size < cells:
@@ -140,17 +163,11 @@
             results = [jnp.where(width == size, v * (1.0 / size), old) for v, old in zip(totals, results)]
         for b in range(blocks):
             Q[pl.ds(pl.multiple_of(r * cells + b * SUB, SUB), SUB), :] = results[b]
-        M[pl.ds(r, 1), :] = totals[0][0:1] * (1.0 / cells)
         ELO[pl.ds(r, 1), :] = results[0][0:1]
         EHI[pl.ds(r, 1), :] = results[blocks - 1][SUB - 1 : SUB]
         return carry
 
-    lax.fori_loop(0, rows, local_average, 0)
-
-    def mean_copy(step):
-        return pltpu.make_async_remote_copy(
-            src_ref=M, dst_ref=MG.at[phi], send_sem=send_mean.at[step], recv_sem=recv_mean.at[step],
-            device_id={"phi": lax.rem(phi + step, nphi)}, device_id_type=MESH)
+    lax.fori_loop(0, rows, local_average, 0, unroll=2)
 
     edge_left = pltpu.make_async_remote_copy(
         src_ref=ELO, dst_ref=ER, send_sem=send_phi.at[0, nvar], recv_sem=recv_phi.at[0, nvar],
@@ -161,8 +178,6 @@
     face_left = pltpu.make_async_remote_copy(
         src_ref=SF, dst_ref=RF, send_sem=send_phi.at[0, nvar + 1], recv_sem=recv_phi.at[0, nvar + 1],
         device_id={"phi": left}, device_id_type=MESH)
-    for step in range(1, nphi):
-        mean_copy(step).start()
     edge_left.start()
     edge_right.start()
     for t in range(tiles):
@@ -209,7 +224,7 @@
 
     for r in (0, 1, rows - 2, rows - 1):
         spread(r)
-    lax.fori_loop(2, rows - 2, lambda r, c: (spread(r), c)[1], 0)
+    lax.fori_loop(2, rows - 2, lambda r, c: (spread(r), c)[1], 0, unroll=2)
 
     down = pltpu.make_async_remote_copy(
         src_ref=H.at[:, pl.ds(2 * ring, 2 * ring)], dst_ref=H.at[:, pl.ds((rows + 2) * ring, 2 * ring)],
@@ -351,6 +366,21 @@
     @pl.when(row < nrow - 1)
     def _():
         up.wait_send()
+
+
+def spill(pieces, conserved, faces, conserved_out, faces_out, sem):
+    fields = conserved.shape[0]
+    size = conserved.shape[1] // pieces
+    copies = []
+    for k in range(fields + faces.shape[0]):
+        source, target, i = (conserved, conserved_out, k) if k < fields else (faces, faces_out, k - fields)
+        for p in range(pieces):
+            where = pl.ds(p * size, size)
+            copies.append(pltpu.make_async_copy(source.at[i, where], target.at[i, where], sem.at[k, p]))
+    for c in copies:
+        c.start()
+    for c in copies:
+        c.wait()
 
 
 def blocked(x):
@@ -379,8 +409,8 @@
     conserved, faces = pl.pallas_call(
         functools.partial(kernel, nrow, nphi, rows, cells, tiles, cycles),
         out_shape=(
-            jax.ShapeDtypeStruct((fields, rows * ring, LANES), f32),
-            jax.ShapeDtypeStruct((nface, rows * ring, LANES), f32),
+            pltpu.VMEM((fields, rows * ring, LANES), f32),
+            pltpu.VMEM((nface, rows * ring, LANES), f32),
         ),
         in_specs=[far, far, far, far],
         out_specs=(near, near),
@@ -416,6 +446,19 @@
         ),
         name="step",
     )(widths, blocked(hydro_vars), blocked(face_b), diffusion)
+    pieces = 2
+    conserved, faces = pl.pallas_call(
+        functools.partial(spill, pieces),
+        out_shape=(
+            jax.ShapeDtypeStruct((fields, rows * ring, LANES), f32),
+            jax.ShapeDtypeStruct((nface, rows * ring, LANES), f32),
+        ),
+        in_specs=[near, near],
+        out_specs=(far, far),
+        scratch_shapes=[pltpu.SemaphoreType.DMA((fields + nface, pieces))],
+        compiler_params=pltpu.CompilerParams(vmem_limit_bytes=1000000),
+        name="spill",
+    )(conserved, faces)
     return unblocked(conserved, rows, cells, theta), unblocked(faces, rows, cells, theta)
 
 

time: 36.6 us -> 28.4 us (0.78)
  the two profiles are of different devices: /device:TPU:27 before, /device:TPU:0 now
where the time goes in v3:
time: 28.4 us; the launch traced here: 28.2 us
  Pallas kernels  27.6 us (97%)
  between operations  0.64 us (2%)
    pallas_call x1, Pallas kernels, body(): pl.pallas_call(functools.partial(kernel, nrow, nphi, rows, cells, tiles,...  24.9 us
    pallas_call x1, Pallas kernels, body(): pl.pallas_call(functools.partial(spill, pieces), out_shape=(jax.ShapeDtyp...  2.67 us

profile of v3, /device:TPU:0, one launch (start us, length us, event | category | flops | bytes accessed | tf_op | source)
XLA Modules:
  0.0 28.2 jit_solution(11795475658878075274)
XLA Ops:
  0.6 24.9 %step.1 = (f32[8,1024,128]{2,1,0:T(8,128)S(1)}, f32[3,1024,128]{2,1,0:T(8,128)S(1)}) custom-call(s32[16]{0:T(128)} %widths_far.1, f32[5,1024,128]{2,1,0:T(8,128)} %bitcast.20, f32[3,1024,128]{2,1,0:T(8,128)} %bitcast.21, f32[5,256]{1,0:T(8,128)} %diffusion_far.1), custom_call_target="tpu_custom_call" | custom-call | tf_op jit(solution)/shard_map/step/pallas_call | solution.py:409
  25.5 2.7 %spill.1 = (f32[8,1024,128]{2,1,0:T(8,128)}, f32[3,1024,128]{2,1,0:T(8,128)}) custom-call(f32[8,1024,128]{2,1,0:T(8,128)S(1)} %get-tuple-element.6.conserved, f32[3,1024,128]{2,1,0:T(8,128)S(1)} %get-tuple-element.7.faces), custom_call_target="tpu_custom_call" | custom-call | tf_op jit(solution)/shard_map/spill/pallas_call | solution.py:450

commit v4 on v3

--- a/solution.py
+++ b/solution.py
@@ -131,7 +131,7 @@
         M[pl.ds(r, 1), :] = value[0:1] * (1.0 / cells)
         return carry
 
-    lax.fori_loop(0, rows, cell_mean, 0, unroll=2)
+    lax.fori_loop(0, rows, cell_mean, 0, unroll=4)
     peers = nphi - 1 + jnp.where(row > 0, 1, 0) + jnp.where(row < nrow - 1, 1, 0)
     pl.semaphore_wait(barrier, peers)
     for step in range(1, nphi):
@@ -224,7 +224,7 @@
 
     for r in (0, 1, rows - 2, rows - 1):
         spread(r)
-    lax.fori_loop(2, rows - 2, lambda r, c: (spread(r), c)[1], 0, unroll=2)
+    lax.fori_loop(2, rows - 2, lambda r, c: (spread(r), c)[1], 0, unroll=4)
 
     down = pltpu.make_async_remote_copy(
         src_ref=H.at[:, pl.ds(2 * ring, 2 * ring)], dst_ref=H.at[:, pl.ds((rows + 2) * ring, 2 * ring)],
@@ -300,7 +300,7 @@
         smooth_row(r)
         return carry
 
-    lax.fori_loop(2, rows - 2, inner_row, 0)
+    lax.fori_loop(2, rows - 2, inner_row, 0, unroll=2)
     for r in (0, 1, rows - 2):
         field_row(r, lambda t, r=r: whole(F, 0, r + 1, t))
 

time: 28.4 us -> 28 us (0.986)
  Pallas kernels: 27.6 us -> 27.2 us
    pallas_call x1, Pallas kernels: 24.9 us -> 24.5 us  [body(): pl.pallas_call(functools.partial(kernel, nrow, nphi, rows, cells, tiles,...]
where the time goes in v4:
time: 28 us; the launch traced here: 27.8 us
  Pallas kernels  27.2 us (97%)
  between operations  0.64 us (2%)
    pallas_call x1, Pallas kernels, body(): pl.pallas_call(functools.partial(kernel, nrow, nphi, rows, cells, tiles,...  24.5 us
    pallas_call x1, Pallas kernels, body(): pl.pallas_call(functools.partial(spill, pieces), out_shape=(jax.ShapeDtyp...  2.67 us

profile of v4, /device:TPU:0, one launch (start us, length us, event | category | flops | bytes accessed | tf_op | source)
XLA Modules:
  0.0 27.8 jit_solution(5934905198295485429)
XLA Ops:
  0.6 24.5 %step.1 = (f32[8,1024,128]{2,1,0:T(8,128)S(1)}, f32[3,1024,128]{2,1,0:T(8,128)S(1)}) custom-call(s32[16]{0:T(128)} %widths_far.1, f32[5,1024,128]{2,1,0:T(8,128)} %bitcast.20, f32[3,1024,128]{2,1,0:T(8,128)} %bitcast.21, f32[5,256]{1,0:T(8,128)} %diffusion_far.1), custom_call_target="tpu_custom_call" | custom-call | tf_op jit(solution)/shard_map/step/pallas_call | solution.py:409
  25.2 2.7 %spill.1 = (f32[8,1024,128]{2,1,0:T(8,128)}, f32[3,1024,128]{2,1,0:T(8,128)}) custom-call(f32[8,1024,128]{2,1,0:T(8,128)S(1)} %get-tuple-element.6.conserved, f32[3,1024,128]{2,1,0:T(8,128)S(1)} %get-tuple-element.7.faces), custom_call_target="tpu_custom_call" | custom-call | tf_op jit(solution)/shard_map/spill/pallas_call | solution.py:450
